TPU v7x, 32 devices: a whole 2x2x4 slice. The times are simulated.
32 devices in a mesh: pipe: 2 (over core), dp: 8 (over z, y), tensor: 2 (over x).
Axes of the slice: x: 2, y: 2, z: 4, core: 2. Of those that a mesh axis runs over, the one named last changes fastest.
Arguments:
- hidden_in: bfloat16 [2, 16, 2, 64, 3584], P('pipe', 'dp'), may hold values from -60 to 60, as said below
- attention_probs: bfloat16 [2, 16, 2, 14, 64, 64], P('pipe', 'dp', None, 'tensor'), may hold values from 0 to 1, as said below
- norm_gain: float32 [2, 3584], P('pipe'), may hold values from 0.5 to 1.5
- value_weight: bfloat16 [2, 3584, 256], P('pipe', None, 'tensor'), may hold values from -0.09375 to 0.09375
- output_weight: bfloat16 [2, 1792, 3584], P('pipe', 'tensor'), may hold values from -0.125 to 0.125
- head_grad: bfloat16 [16, 2, 64, 3584], P('dp', 'tensor'), may hold values from -16 to 16
- policy_logprob: float32 [16, 2, 64], P('dp'), may hold values from -3 to -0.2
- reference_logprob: float32 [16, 2], P('dp'), may hold values from -96 to -12.8
- sequence_bounds: int32 [16, 3], P('dp'), may hold values from 1 to 64, as said below
Outputs:
- section_cotangent: bfloat16 [2, 16, 2, 64, 3584], P('pipe', 'dp', 'tensor')
- value_gradient: float32 [2, 3584, 256], P('pipe', 'dp', 'tensor')
- output_gradient: float32 [2, 3584, 1792], P('pipe', 'dp', 'tensor')
- gain_gradient: float32 [2, 3584], P('pipe', 'dp')
Inputs may be any that keep to these rules, and one draw needn't show every extreme that they name: `sequence_bounds`: entry 0 is the prompt length, shared by the two sequences of a pair; a sequence's response is the positions from entry 0 up to its end (entry 1 for the chosen, entry 2 for the rejected sequence), and holds one position or more. `attention_probs`: each row is a causal attention distribution: zero above the diagonal, summing to one before rounding. `hidden_in`: activations of varying size from token to token.
All inputs are finite; a program needn't handle non-finite values.
Results may differ from a plain program's by a relative error of at most 0.017.
Values may be sent and summed in bfloat16 or wider, within the bound.
A program may use at most 128 MiB of HBM per device.

v0:
```python
import jax
import jax.numpy as jnp
from jax import lax
from jax.sharding import PartitionSpec as P

HEAD_DIM = 128
EPSILON = 1e-06
DPO_BETA = 0.25
LIKELIHOOD_COEF = 0.2


def shifted(block, axis, distance):
    devices = range(lax.axis_size(axis))
    route = [(i - distance, i) for i in devices if i - distance in devices]
    return lax.ppermute(block, axis, route)


def body(
    hidden_in,
    attention_probs,
    norm_gain,
    value_weight,
    output_weight,
    head_grad,
    policy_logprob,
    reference_logprob,
    sequence_bounds,
):
    section_count = lax.axis_size("pipe")
    section_index = lax.axis_index("pipe")
    tensor_index = lax.axis_index("tensor")
    micro_count = hidden_in.shape[1]
    sequence_length = hidden_in.shape[3]
    model_width = hidden_in.shape[4]
    value_columns = value_weight.shape[2]
    value_heads = value_columns // HEAD_DIM
    local_heads = attention_probs.shape[3]
    group_size = local_heads // value_heads
    mixed_columns = output_weight.shape[1]
    own_rows = 2 // lax.axis_size("tensor")
    gain_vector = norm_gain[0]
    value_matrix = value_weight[0]
    output_matrix = output_weight[0]
    saved_inputs = hidden_in[0]
    saved_pattern = attention_probs[0]
    positions = jnp.arange(sequence_length, dtype=jnp.int32)
    response_bool = (positions[None, None, :] >= sequence_bounds[:, 0:1, None]) & (
        positions[None, None, :] < sequence_bounds[:, 1:3, None]
    )
    response_mask = response_bool.astype(jnp.float32)
    sequence_logprob = jnp.sum(response_mask * policy_logprob, axis=-1)
    margin = DPO_BETA * (
        sequence_logprob[:, 0]
        - reference_logprob[:, 0]
        - (sequence_logprob[:, 1] - reference_logprob[:, 1])
    )
    weight_pair = jax.nn.sigmoid(-margin)
    local_count = jnp.sum(response_bool[:, 0, :].astype(jnp.int32))
    chosen_total = lax.psum(local_count, "dp")
    pair_total = micro_count * lax.axis_size("dp")
    likelihood_scale = (
        LIKELIHOOD_COEF * jnp.asarray(pair_total, jnp.float32) / chosen_total.astype(jnp.float32)
    )
    chosen_weight = (
        -DPO_BETA * weight_pair[:, None] * response_mask[:, 0]
        - likelihood_scale * response_mask[:, 0]
    )
    rejected_weight = DPO_BETA * weight_pair[:, None] * response_mask[:, 1]
    token_weight = jnp.stack([chosen_weight, rejected_weight], axis=1)
    full_head_grad = lax.all_gather(head_grad, "tensor", axis=1, tiled=True)
    top_cotangent = (token_weight[..., None] * full_head_grad.astype(jnp.float32)).astype(
        jnp.bfloat16
    )
    send_rows = 2

    def local_backward(operands):
        inputs, pattern, upstream = operands
        input_float = inputs.astype(jnp.float32)
        inverse_rms = lax.rsqrt(
            jnp.mean(input_float * input_float, axis=-1, keepdims=True) + EPSILON
        )
        normed = (input_float * inverse_rms * gain_vector).astype(jnp.bfloat16)
        values = jnp.dot(normed, value_matrix, preferred_element_type=jnp.float32).astype(
            jnp.bfloat16
        )
        grouped = pattern.reshape(2, value_heads, group_size, sequence_length, sequence_length)
        values_heads = values.reshape(2, sequence_length, value_heads, HEAD_DIM)
        mixed = jnp.einsum(
            "ckgst,ctke->cskge", grouped, values_heads, preferred_element_type=jnp.float32
        )
        mixed = mixed.astype(jnp.bfloat16).reshape(2, sequence_length, mixed_columns)
        mixed_grad = jnp.einsum(
            "csd,hd->csh", upstream, output_matrix, preferred_element_type=jnp.float32
        ).astype(jnp.bfloat16)
        mixed_heads = mixed_grad.reshape(2, sequence_length, value_heads, group_size, HEAD_DIM)
        values_grad = jnp.einsum(
            "ckgst,cskge->ctke", grouped, mixed_heads, preferred_element_type=jnp.float32
        )
        values_grad = values_grad.astype(jnp.bfloat16).reshape(2, sequence_length, value_columns)
        partial_value = jnp.einsum(
            "csk,dk->csd", values_grad, value_matrix, preferred_element_type=jnp.float32
        )
        return (partial_value, inverse_rms, normed, mixed, values_grad)

    def skipped(operands):
        return (
            jnp.zeros((2, sequence_length, model_width), jnp.float32),
            jnp.zeros((2, sequence_length, 1), jnp.float32),
            jnp.zeros((2, sequence_length, model_width), jnp.bfloat16),
            jnp.zeros((2, sequence_length, mixed_columns), jnp.bfloat16),
            jnp.zeros((2, sequence_length, value_columns), jnp.bfloat16),
        )

    def place(buffer, value, slot_index, active):
        previous = lax.dynamic_index_in_dim(buffer, slot_index, 0, keepdims=False)
        return lax.dynamic_update_index_in_dim(
            buffer, jnp.where(active, value, previous), slot_index, 0
        )

    def turn_step(turn, state_tuple):
        outgoing, outputs, gain_total, kept_state = state_tuple
        incoming = shifted(outgoing, "pipe", -1)
        micro_index = turn - (section_count - 1 - section_index)
        active = (micro_index >= 0) & (micro_index < micro_count)
        slot_index = jnp.clip(micro_index, 0, micro_count - 1)
        top_slice = lax.dynamic_index_in_dim(top_cotangent, slot_index, 0, keepdims=False)
        upstream = jnp.where(section_index == section_count - 1, top_slice, incoming)
        inputs = lax.dynamic_index_in_dim(saved_inputs, slot_index, 0, keepdims=False)
        pattern = lax.dynamic_index_in_dim(saved_pattern, slot_index, 0, keepdims=False)
        partial_value, inverse_rms, normed, mixed, values_grad = lax.cond(
            active, local_backward, skipped, (inputs, pattern, upstream)
        )
        normed_grad = lax.psum(partial_value.astype(jnp.bfloat16), "tensor").astype(jnp.float32)
        input_float = inputs.astype(jnp.float32)
        scaled = normed_grad * gain_vector
        cubed = inverse_rms * inverse_rms * inverse_rms
        input_grad = inverse_rms * scaled - input_float * cubed * jnp.mean(
            input_float * scaled, axis=-1, keepdims=True
        )
        new_rows = (upstream.astype(jnp.float32) + input_grad).astype(jnp.bfloat16)
        gain_terms = jnp.sum(normed_grad * input_float * inverse_rms, axis=(0, 1))
        gain_total = gain_total + jnp.where(active, gain_terms, 0.0)
        outputs = place(outputs, new_rows, slot_index, active)
        saved_upstream, saved_mixed, saved_normed, saved_values = kept_state
        kept_state = (
            place(saved_upstream, upstream, slot_index, active),
            place(saved_mixed, mixed, slot_index, active),
            place(saved_normed, normed, slot_index, active),
            place(saved_values, values_grad, slot_index, active),
        )
        return (new_rows, outputs, gain_total, kept_state)

    kept_state = (
        jnp.zeros((micro_count, 2, sequence_length, model_width), jnp.bfloat16),
        jnp.zeros((micro_count, 2, sequence_length, mixed_columns), jnp.bfloat16),
        jnp.zeros((micro_count, 2, sequence_length, model_width), jnp.bfloat16),
        jnp.zeros((micro_count, 2, sequence_length, value_columns), jnp.bfloat16),
    )
    initial = (
        jnp.zeros((send_rows, sequence_length, model_width), jnp.bfloat16),
        jnp.zeros((micro_count, send_rows, sequence_length, model_width), jnp.bfloat16),
        jnp.zeros((model_width,), jnp.float32),
        kept_state,
    )
    final_state = lax.fori_loop(0, section_count + micro_count - 1, turn_step, initial)
    outgoing, outputs, gain_total, kept_state = final_state
    own_output = lax.dynamic_slice_in_dim(outputs, tensor_index * own_rows, own_rows, 1)
    saved_upstream, saved_mixed, saved_normed, saved_values = kept_state
    value_part = jnp.einsum(
        "mcsd,mcsk->dk", saved_normed, saved_values, preferred_element_type=jnp.float32
    )
    mixed_part = jnp.einsum(
        "mcsd,mcsh->dh", saved_upstream, saved_mixed, preferred_element_type=jnp.float32
    )
    grad_share = lax.psum_scatter(
        jnp.concatenate([value_part, mixed_part], axis=1), "dp", scatter_dimension=0, tiled=True
    )
    gain_rows = lax.psum_scatter(gain_total, "dp", scatter_dimension=0, tiled=True)
    value_share = grad_share[:, :value_columns]
    mixed_share = grad_share[:, value_columns:]
    return (own_output[None], value_share[None], mixed_share[None], gain_rows[None])


def solution(mesh):
    in_specs = (
        P("pipe", "dp", None, None, None),
        P("pipe", "dp", None, "tensor", None, None),
        P("pipe", None),
        P("pipe", None, "tensor"),
        P("pipe", "tensor", None),
        P("dp", "tensor", None, None),
        P("dp", None, None),
        P("dp", None),
        P("dp", None),
    )
    out_specs = (
        P("pipe", "dp", "tensor", None, None),
        P("pipe", "dp", "tensor"),
        P("pipe", "dp", "tensor"),
        P("pipe", "dp"),
    )
    return jax.shard_map(body, mesh=mesh, in_specs=in_specs, out_specs=out_specs, check_vma=False)
```

profile of v0, /device:TPU:0, one launch (start us, length us, event | category | flops | bytes accessed | tf_op | source)
XLA Modules:
  0.0 537.4 jit_solution(17916456132910922328)
XLA Ops:
  11.0 13.7 %psum.20 = s32[]{:T(128)} all-reduce(s32[]{:T(128)} %fusion.37), channel_id=1, replica_groups=mesh['pipe'=2,'dp'=8,'tensor'=2] {'dp'}, use_global_device_ids=true, to_apply=%region_2.0 | all-reduce | flops 1 | bytes 8 | tf_op jit(solution)/shard_map/psum | solution.py:59
  25.4 2.0 copy.35
  27.8 14.7 %all-gather.2.cloned.1.call-done = bf16[2,2,64,3584]{3,2,1,0:T(8,128)(2,1)} async-done(((bf16[2,1,64,3584]{3,2,1,0:T(8,128)(2,1)}), bf16[2,2,64,3584]{3,2,1,0:T(8,128)(2,1)}) %all-gather.2.cloned.1.call-update) | async-done | bytes 1835024 | tf_op jit(solution)/shard_map/all_gather | solution.py:70
  42.5 3.2 multiply_convert_fusion
  46.5 1.4 broadcast.117.clone2
  47.9 1.4 broadcast.117.clone
  49.3 1.4 broadcast.117
  50.7 201.7 %while.28 = (s32[]{:T(128)}, bf16[2,64,3584]{2,1,0:T(8,128)(2,1)}, bf16[2,2,64,3584]{3,2,1,0:T(8,128)(2,1)}, f32[3584]{0:T(1024)S(1)}, bf16[2,2,64,3584]{3,2,0,1...) while((s32[]{:T(128)}, bf16[2,64,3584]{2,1,0:T(8,128)(2,1)}, ...), condition=%wide.region_10.11_spmd.clone, body=%wide.region_3.10_spmd.clone.sunk | while | flops 1100947072 | bytes 77010576 | solution.py:165
  50.7 1.3 collective-permute-start
  53.0 2.2 constant_dynamic-slice_fusion.13
  56.5 2.3 constant_dynamic-slice_fusion.10
  60.1 2.6 bitcast_dynamic-update-slice_fusion.10
  62.6 1.7 conditional.3
  66.1 2.4 bitcast_dynamic-update-slice_fusion.13
  68.5 44.5 %all-reduce.3.cloned.1.call-done = bf16[2,64,3584]{2,1,0:T(8,128)(2,1)} async-done(((bf16[2,64,3584]{2,1,0:T(8,128)(2,1)}), bf16[2,64,3584]{2,1,0:T(8,128)(2,1)}) %all-reduce.3.cloned.1.call-update) | async-done | bytes 917520 | tf_op jit(solution)/shard_map/while/body/eval_jaxpr/psum | solution.py:133
  113.0 2.1 fusion.49
  115.1 2.2 bitcast_dynamic-update-slice_fusion.11
  118.6 1.3 collective-permute-start
  120.9 2.2 constant_dynamic-slice_fusion.13
  124.3 2.3 constant_dynamic-slice_fusion.10
  127.9 2.6 bitcast_dynamic-update-slice_fusion.10
  130.5 11.5 %conditional.3 = (bf16[2,64,3584]{2,1,0:T(8,128)(2,1)S(1)}, f32[2,64,1]{1,0,2:T(2,128)S(1)}, bf16[2,64,3584]{2,1,0:T(8,128)(2,1)}, bf16[2,64,896]{2,1,0:T(8,128)...) conditional(s32[]{:T(128)} %convert_element_type.187, () %tuple.75, ...), branch_computations={%region_4.4_spmd, %region_5.6_spmd} | conditional | flops 1089798656 | bytes 16856664 | solution.py:130
  130.5 5.0 fusion.9
  137.9 2.0 fusion.8
  140.4 1.6 fusion.16
  144.6 2.6 bitcast_dynamic-update-slice_fusion.13
  147.3 33.5 %all-reduce.3.cloned.1.call-done = bf16[2,64,3584]{2,1,0:T(8,128)(2,1)} async-done(((bf16[2,64,3584]{2,1,0:T(8,128)(2,1)}), bf16[2,64,3584]{2,1,0:T(8,128)(2,1)}) %all-reduce.3.cloned.1.call-update) | async-done | bytes 917520 | tf_op jit(solution)/shard_map/while/body/eval_jaxpr/psum | solution.py:133
  180.8 2.1 fusion.49
  182.9 2.2 bitcast_dynamic-update-slice_fusion.11
  188.7 2.2 constant_dynamic-slice_fusion.13
  192.2 2.3 constant_dynamic-slice_fusion.10
  195.7 2.5 bitcast_dynamic-update-slice_fusion.10
  198.2 11.5 %conditional.3 = (bf16[2,64,3584]{2,1,0:T(8,128)(2,1)S(1)}, f32[2,64,1]{1,0,2:T(2,128)S(1)}, bf16[2,64,3584]{2,1,0:T(8,128)(2,1)}, bf16[2,64,896]{2,1,0:T(8,128)...) conditional(s32[]{:T(128)} %convert_element_type.187, () %tuple.75, ...), branch_computations={%region_4.4_spmd, %region_5.6_spmd} | conditional | flops 1089798656 | bytes 16856664 | solution.py:130
  198.3 5.0 fusion.9
  205.7 2.0 fusion.8
  208.2 1.6 fusion.16
  212.4 2.6 bitcast_dynamic-update-slice_fusion.13
  215.1 33.1 %all-reduce.3.cloned.1.call-done = bf16[2,64,3584]{2,1,0:T(8,128)(2,1)} async-done(((bf16[2,64,3584]{2,1,0:T(8,128)(2,1)}), bf16[2,64,3584]{2,1,0:T(8,128)(2,1)}) %all-reduce.3.cloned.1.call-update) | async-done | bytes 917520 | tf_op jit(solution)/shard_map/while/body/eval_jaxpr/psum | solution.py:133
  248.1 2.1 fusion.49
  250.2 2.1 bitcast_dynamic-update-slice_fusion.11
  252.4 1.9 convolution_bitcast_fusion.2
  254.3 8.1 %convolution_bitcast_fusion.1 = f32[3584,896]{0,1:T(8,128)} fusion(bf16[2,2,64,3584]{3,2,0,1:T(8,128)(2,1)} %get-tuple-element.398, bf16[2,2,64,896]{3,2,0,1:T(8,128)(2,1)} %get-tuple-element.399), kind=kOutput, calls=%fused_computation.63 | convolution fusion | flops 1644167168 | bytes 15138816 | tf_op jit(solution)/shard_map/mcsd,mcsh->dh/dot_general | solution.py:172
  262.4 10.8 %pad_maximum_fusion = f32[3584,1024]{0,1:T(8,128)} fusion(f32[3584,896]{0,1:T(8,128)} %convolution_bitcast_fusion.1, f32[3584,128]{0,1:T(8,128)S(1)} %convolution_bitcast_fusion.2), kind=kLoop, calls=%fused_computation.62 | loop fusion | flops 3670016 | bytes 29360128 | tf_op jit(solution)/shard_map/concatenate | solution.py:176
  273.2 15.3 %copy.47 = f32[3584,1024]{1,0:T(8,128)} copy(f32[3584,1024]{0,1:T(8,128)} %pad_maximum_fusion) | data formatting | bytes 29360128
  290.5 39.3 %all-reduce = f32[3584]{0:T(1024)S(1)} all-reduce(f32[3584]{0:T(1024)S(1)} %get-tuple-element.400), channel_id=3, replica_groups=mesh['pipe'=2,'dp'=8,'tensor'=2] {'dp'}, use_global_device_ids=true, to_apply=%region_12.13.clone | all-reduce | flops 3584 | bytes 28672
  330.4 2.2 dynamic-slice_bitcast_fusion.1
  332.6 193.3 %reduce-scatter.4.cloned.1.call-done = f32[448,1024]{1,0:T(8,128)} async-done(((f32[3584,1024]{1,0:T(8,128)}), f32[448,1024]{1,0:T(8,128)}) %reduce-scatter.4.cloned.1.call-update) | async-done | bytes 1835024
  529.3 1.6 copy.41
  (130 shorter events, 39.1 us)
Async XLA Ops:
  7.2 20.3 %copy-start.7 = (f32[2,2]{1,0:T(2,128)S(1)}, f32[2,2]{1,0:T(2,128)}, u32[]{:S(2)}) copy-start(f32[2,2]{1,0:T(2,128)} %param.20) | copy-start | bytes 52
  7.2 35.3 %all-gather.2.cloned.1.call-start = ((), (), s32[]{:S(2)}) async-start(), calls=%async_computation.1 | async-start | bytes 2752512 | tf_op jit(solution)/shard_map/all_gather | solution.py:70
  47.9 2.8 copy-start.6
  50.7 62.3 %all-reduce.3.cloned.1.call-start = ((), (), s32[]{:S(2)}) async-start(), calls=%async_computation.3 | async-start | bytes 1835008 | tf_op jit(solution)/shard_map/while/body/eval_jaxpr/psum | solution.py:133
  50.7 9.3 %collective-permute-start = (bf16[2,64,3584]{2,1,0:T(8,128)(2,1)S(1)}, bf16[2,64,3584]{2,1,0:T(8,128)(2,1)}, u32[]{:S(2)}, u32[]{:S(2)}) collective-permute-start(bf16[2,64,3584]{2,1,0:T(8,128)(2,1)S(1)} %broadcast_select_fusion.2), channel_id=1, source_target_pairs={{16,0},{17,1},{18,2},{19,3},{20,4},{21,5},{22,6},{23,7},{24,8},{25... | collective-permute-start | bytes 2752520 | tf_op jit(solution)/shard_map/while/body/eval_jaxpr/ppermute | solution.py:15
  56.5 3.6 copy-start.4
  64.3 1.0 copy-start.3
  65.3 47.7 %copy-start = (bf16[2,2,64,3584]{3,2,1,0:T(8,128)(2,1)S(1)}, bf16[2,2,64,3584]{3,2,1,0:T(8,128)(2,1)}, u32[]{:S(2)}) copy-start(bf16[2,2,64,3584]{3,2,1,0:T(8,128)(2,1)} %get-tuple-element.700) | copy-start | bytes 5505028 | tf_op jit(solution)/shard_map/while
  113.0 2.1 copy-start.1
  113.0 2.1 copy-start.2
  117.3 63.5 %all-reduce.3.cloned.1.call-start = ((), (), s32[]{:S(2)}) async-start(), calls=%async_computation.3 | async-start | bytes 1835008 | tf_op jit(solution)/shard_map/while/body/eval_jaxpr/psum | solution.py:133
  118.6 9.3 %collective-permute-start = (bf16[2,64,3584]{2,1,0:T(8,128)(2,1)S(1)}, bf16[2,64,3584]{2,1,0:T(8,128)(2,1)}, u32[]{:S(2)}, u32[]{:S(2)}) collective-permute-start(bf16[2,64,3584]{2,1,0:T(8,128)(2,1)S(1)} %broadcast_select_fusion.2), channel_id=1, source_target_pairs={{16,0},{17,1},{18,2},{19,3},{20,4},{21,5},{22,6},{23,7},{24,8},{25... | collective-permute-start | bytes 2752520 | tf_op jit(solution)/shard_map/while/body/eval_jaxpr/ppermute | solution.py:15
  124.3 3.6 copy-start.4
  130.5 5.0 copy-start.5
  142.0 1.0 copy-start.3
  143.0 37.9 %copy-start = (bf16[2,2,64,3584]{3,2,1,0:T(8,128)(2,1)S(1)}, bf16[2,2,64,3584]{3,2,1,0:T(8,128)(2,1)}, u32[]{:S(2)}) copy-start(bf16[2,2,64,3584]{3,2,1,0:T(8,128)(2,1)} %get-tuple-element.700) | copy-start | bytes 5505028 | tf_op jit(solution)/shard_map/while
  180.8 2.1 copy-start.1
  180.8 2.1 copy-start.2
  185.1 63.0 %all-reduce.3.cloned.1.call-start = ((), (), s32[]{:S(2)}) async-start(), calls=%async_computation.3 | async-start | bytes 1835008 | tf_op jit(solution)/shard_map/while/body/eval_jaxpr/psum | solution.py:133
  186.4 9.3 %collective-permute-start = (bf16[2,64,3584]{2,1,0:T(8,128)(2,1)S(1)}, bf16[2,64,3584]{2,1,0:T(8,128)(2,1)}, u32[]{:S(2)}, u32[]{:S(2)}) collective-permute-start(bf16[2,64,3584]{2,1,0:T(8,128)(2,1)S(1)} %broadcast_select_fusion.2), channel_id=1, source_target_pairs={{16,0},{17,1},{18,2},{19,3},{20,4},{21,5},{22,6},{23,7},{24,8},{25... | collective-permute-start | bytes 2752520 | tf_op jit(solution)/shard_map/while/body/eval_jaxpr/ppermute | solution.py:15
  192.1 3.6 copy-start.4
  198.2 5.0 copy-start.5
  209.8 1.0 copy-start.3
  210.7 37.4 %copy-start = (bf16[2,2,64,3584]{3,2,1,0:T(8,128)(2,1)S(1)}, bf16[2,2,64,3584]{3,2,1,0:T(8,128)(2,1)}, u32[]{:S(2)}) copy-start(bf16[2,2,64,3584]{3,2,1,0:T(8,128)(2,1)} %get-tuple-element.700) | copy-start | bytes 5505028 | tf_op jit(solution)/shard_map/while
  248.1 2.1 copy-start.1
  248.1 2.1 copy-start.2
  252.4 273.5 %reduce-scatter.4.cloned.1.call-start = ((), (), s32[]{:S(2)}) async-start(), calls=%async_computation.2 | async-start | bytes 16515072
  288.6 0.7 copy-start.8
  527.0 1.5 slice-start
Sparse Core Ops, SparseCore 0:
  9.5 32.8 all-gather.1
  65.4 47.5 all-reduce.2
  143.1 37.6 all-reduce.2
  210.9 37.2 all-reduce.2
  288.7 237.1 reduce-scatter.3
where the time goes:
time: 539 us; the launch traced here: 537 us
  waiting for transfers between devices  320 us (59%)
  local copies, waits for them, and re-layouts  62.1 us (12%)
  other arithmetic  53.8 us (10%)
  blocking collectives  53 us (10%)
  matrix products  29 us (5%)
  between operations  15.1 us (3%)
    unnamed x3, waiting for transfers between devices  194 us
    psum x3, waiting for transfers between devices, turn_step(): lax.psum(partial_value.astype(jnp.bfloat16), 'tensor').astype(jnp.float32)  111 us
    unnamed x1, blocking collectives  39.3 us
    dynamic_update_slice x15, other arithmetic, place(): lax.dynamic_update_index_in_dim(buffer, jnp.where(active, value, previous...  25.9 us
    unnamed x14, local copies, waits for them, and re-layouts  22.6 us
    dynamic_slice x15, local copies, waits for them, and re-layouts, place(): previous = lax.dynamic_index_in_dim(buffer, slot_index, 0, keepdims=False)  20.1 us
    all_gather x1, waiting for transfers between devices, body(): full_head_grad = lax.all_gather(head_grad, 'tensor', axis=1, tiled=True)  14.7 us
    psum x1, blocking collectives, body(): chosen_total = lax.psum(local_count, 'dp')  13.7 us
  transfers between devices with their start and end apart: 8, of which 5 were waited for; matrix products, arithmetic and copies ran while one was open for 8% of the time, Pallas kernels for 0%

commit v1 on v0

--- a/solution.py
+++ b/solution.py
@@ -130,7 +130,9 @@
         partial_value, inverse_rms, normed, mixed, values_grad = lax.cond(
             active, local_backward, skipped, (inputs, pattern, upstream)
         )
-        normed_grad = lax.psum(partial_value.astype(jnp.bfloat16), "tensor").astype(jnp.float32)
+        normed_grad = jnp.sum(
+            lax.all_gather(partial_value.astype(jnp.bfloat16), "tensor"), axis=0
+        ).astype(jnp.float32)
         input_float = inputs.astype(jnp.float32)
         scaled = normed_grad * gain_vector
         cubed = inverse_rms * inverse_rms * inverse_rms

time: 539 us -> 520 us (0.965)
  waiting for transfers between devices: 320 us -> 297 us
    psum x3 -> x0, waiting for transfers between devices: 111 us -> none  [turn_step(): lax.psum(partial_value.astype(jnp.bfloat16), 'tensor').astype(jnp.float32)]
    all_gather x0 -> x3, waiting for transfers between devices: none -> 88.6 us  [turn_step(): lax.all_gather(partial_value.astype(jnp.bfloat16), 'tensor')]
    dynamic_slice x15 -> x12, local copies, waits for them, and re-layouts: 20.1 us -> 12.7 us  [place(): previous = lax.dynamic_index_in_dim(buffer, slot_index, 0, keepdims=False)]
    reduce_sum x0 -> x3, other arithmetic: none -> 5.68 us  [turn_step(): jnp.sum(lax.all_gather(partial_value.astype(jnp.bfloat16), 'tensor'), axi...]
    unnamed x14 -> x18, local copies, waits for them, and re-layouts: 22.6 us -> 23.6 us
  transfers between devices with their start and end apart: 8 -> 8, of which waited for: 5 -> 5; matrix products, arithmetic and copies ran while one was open for 8% -> 7% of each run, Pallas kernels for 0% -> 0%
where the time goes in v1:
time: 520 us; the launch traced here: 518 us
  waiting for transfers between devices  297 us (57%)
  local copies, waits for them, and re-layouts  61.9 us (12%)
  other arithmetic  58.4 us (11%)
  blocking collectives  53 us (10%)
  matrix products  28 us (5%)
  between operations  15.2 us (3%)
    unnamed x3, waiting for transfers between devices  194 us
    all_gather x3, waiting for transfers between devices, turn_step(): lax.all_gather(partial_value.astype(jnp.bfloat16), 'tensor')  88.6 us
    unnamed x1, blocking collectives  39.3 us
    dynamic_update_slice x15, other arithmetic, place(): lax.dynamic_update_index_in_dim(buffer, jnp.where(active, value, previous...  24.7 us
    unnamed x18, local copies, waits for them, and re-layouts  23.6 us
    all_gather x1, waiting for transfers between devices, body(): full_head_grad = lax.all_gather(head_grad, 'tensor', axis=1, tiled=True)  14.7 us
    psum x1, blocking collectives, body(): chosen_total = lax.psum(local_count, 'dp')  13.7 us
    dynamic_slice x12, local copies, waits for them, and re-layouts, place(): previous = lax.dynamic_index_in_dim(buffer, slot_index, 0, keepdims=False)  12.7 us
  transfers between devices with their start and end apart: 8, of which 5 were waited for; matrix products, arithmetic and copies ran while one was open for 7% of the time, Pallas kernels for 0%

profile of v1, /device:TPU:0, one launch (start us, length us, event | category | flops | bytes accessed | tf_op | source)
XLA Modules:
  0.0 518.2 jit_solution(13293528435983367731)
XLA Ops:
  11.0 13.7 %psum.7 = s32[]{:T(128)} all-reduce(s32[]{:T(128)} %fusion.37), channel_id=1, replica_groups=mesh['pipe'=2,'dp'=8,'tensor'=2] {'dp'}, use_global_device_ids=true, to_apply=%region_2.0 | all-reduce | flops 1 | bytes 8 | tf_op jit(solution)/shard_map/psum | solution.py:59
  25.4 2.0 copy.35
  27.8 14.7 %all-gather.7.cloned.1.call-done = bf16[2,2,64,3584]{3,2,1,0:T(8,128)(2,1)} async-done(((bf16[2,1,64,3584]{3,2,1,0:T(8,128)(2,1)}), bf16[2,2,64,3584]{3,2,1,0:T(8,128)(2,1)}) %all-gather.7.cloned.1.call-update) | async-done | bytes 1835024 | tf_op jit(solution)/shard_map/all_gather | solution.py:70
  42.5 3.2 multiply_convert_fusion
  46.4 1.4 broadcast.118.clone2
  49.2 1.4 broadcast.118
  50.6 181.0 %while.28 = (s32[]{:T(128)}, bf16[2,64,3584]{2,1,0:T(8,128)(2,1)}, bf16[2,2,64,3584]{3,2,1,0:T(8,128)(2,1)}, f32[3584]{0:T(1024)S(1)}, bf16[2,2,64,3584]{3,2,0,1...) while((s32[]{:T(128)}, bf16[2,64,3584]{2,1,0:T(8,128)(2,1)}, ...), condition=%wide.region_10.11_spmd.clone, body=%wide.region_3.10_spmd.clone.sunk | while | flops 1100947072 | bytes 97195200 | solution.py:167
  52.0 2.3 constant_dynamic-slice_fusion.9
  57.4 1.7 bitcast_dynamic-update-slice_fusion.10
  60.3 2.7 conditional.3
  65.9 37.1 %all-gather.9.cloned.1.call-done = bf16[4,64,3584]{2,1,0:T(8,128)(2,1)} async-done(((bf16[2,64,3584]{2,1,0:T(8,128)(2,1)}), bf16[4,64,3584]{2,1,0:T(8,128)(2,1)}) %all-gather.9.cloned.1.call-update) | async-done | bytes 1835024 | tf_op jit(solution)/shard_map/while/body/eval_jaxpr/all_gather | solution.py:134
  102.9 1.9 reduce_sum.87
  104.9 2.1 fusion.49
  106.9 3.4 bitcast_dynamic-update-slice_fusion.11
  112.9 2.3 constant_dynamic-slice_fusion.9
  118.3 1.7 bitcast_dynamic-update-slice_fusion.10
  121.3 11.8 %conditional.3 = (bf16[2,64,3584]{2,1,0:T(8,128)(2,1)}, f32[2,64,1]{1,0,2:T(2,128)S(1)}, bf16[2,64,3584]{2,1,0:T(8,128)(2,1)}, bf16[2,64,896]{2,1,0:T(8,128)(2,1...) conditional(s32[]{:T(128)} %convert_element_type.199, () %tuple.79, ...), branch_computations={%region_4.4_spmd, %region_5.6_spmd} | conditional | flops 1089798656 | bytes 16857172 | solution.py:130
  121.3 5.0 fusion.9
  128.7 1.8 fusion.8
  131.0 2.1 fusion.16
  134.0 1.4 bitcast_dynamic-update-slice_fusion.14
  135.5 2.4 bitcast_dynamic-update-slice_fusion.13
  137.8 26.0 %all-gather.9.cloned.1.call-done = bf16[4,64,3584]{2,1,0:T(8,128)(2,1)} async-done(((bf16[2,64,3584]{2,1,0:T(8,128)(2,1)}), bf16[4,64,3584]{2,1,0:T(8,128)(2,1)}) %all-gather.9.cloned.1.call-update) | async-done | bytes 1835024 | tf_op jit(solution)/shard_map/while/body/eval_jaxpr/all_gather | solution.py:134
  163.9 1.9 reduce_sum.87
  165.8 2.1 fusion.49
  167.8 3.4 bitcast_dynamic-update-slice_fusion.11
  173.8 2.3 constant_dynamic-slice_fusion.9
  179.2 1.7 bitcast_dynamic-update-slice_fusion.10
  182.2 11.8 %conditional.3 = (bf16[2,64,3584]{2,1,0:T(8,128)(2,1)}, f32[2,64,1]{1,0,2:T(2,128)S(1)}, bf16[2,64,3584]{2,1,0:T(8,128)(2,1)}, bf16[2,64,896]{2,1,0:T(8,128)(2,1...) conditional(s32[]{:T(128)} %convert_element_type.199, () %tuple.79, ...), branch_computations={%region_4.4_spmd, %region_5.6_spmd} | conditional | flops 1089798656 | bytes 16857172 | solution.py:130
  182.2 5.0 fusion.9
  189.6 1.8 fusion.8
  191.9 2.1 fusion.16
  194.9 1.4 bitcast_dynamic-update-slice_fusion.14
  196.4 2.4 bitcast_dynamic-update-slice_fusion.13
  198.8 25.5 %all-gather.9.cloned.1.call-done = bf16[4,64,3584]{2,1,0:T(8,128)(2,1)} async-done(((bf16[2,64,3584]{2,1,0:T(8,128)(2,1)}), bf16[4,64,3584]{2,1,0:T(8,128)(2,1)}) %all-gather.9.cloned.1.call-update) | async-done | bytes 1835024 | tf_op jit(solution)/shard_map/while/body/eval_jaxpr/all_gather | solution.py:134
  224.3 1.9 reduce_sum.87
  226.2 2.1 fusion.49
  228.3 3.3 bitcast_dynamic-update-slice_fusion.11
  231.6 2.1 convolution_bitcast_fusion.2
  233.7 6.5 %convolution_bitcast_fusion.1 = f32[3584,896]{0,1:T(8,128)} fusion(bf16[2,2,64,3584]{3,2,0,1:T(8,128)(2,1)S(1)} %copy-done.6, bf16[2,2,64,896]{3,2,0,1:T(8,128)(2,1)S(1)} %get-tuple-element.415), kind=kOutput, calls=%fused_computation.63 | convolution fusion | flops 1644167168 | bytes 15138816 | tf_op jit(solution)/shard_map/mcsd,mcsh->dh/dot_general | solution.py:174
  240.2 10.8 %pad_maximum_fusion = f32[3584,1024]{0,1:T(8,128)} fusion(f32[3584,896]{0,1:T(8,128)} %convolution_bitcast_fusion.1, f32[3584,128]{0,1:T(8,128)S(1)} %convolution_bitcast_fusion.2), kind=kLoop, calls=%fused_computation.62 | loop fusion | flops 3670016 | bytes 29360128 | tf_op jit(solution)/shard_map/concatenate | solution.py:178
  251.0 15.3 %copy.47 = f32[3584,1024]{1,0:T(8,128)} copy(f32[3584,1024]{0,1:T(8,128)} %pad_maximum_fusion) | data formatting | bytes 29360128
  268.2 39.3 %all-reduce = f32[3584]{0:T(1024)S(1)} all-reduce(f32[3584]{0:T(1024)S(1)} %get-tuple-element.416), channel_id=4, replica_groups=mesh['pipe'=2,'dp'=8,'tensor'=2] {'dp'}, use_global_device_ids=true, to_apply=%region_12.13.clone | all-reduce | flops 3584 | bytes 28672
  308.2 2.2 dynamic-slice_bitcast_fusion.1
  310.4 193.3 %reduce-scatter.4.cloned.1.call-done = f32[448,1024]{1,0:T(8,128)} async-done(((f32[3584,1024]{1,0:T(8,128)}), f32[448,1024]{1,0:T(8,128)}) %reduce-scatter.4.cloned.1.call-update) | async-done | bytes 1835024
  505.6 2.7 slice.49
  508.2 1.8 copy.62
  510.1 1.6 copy.41
  (139 shorter events, 42.7 us)
Async XLA Ops:
  7.2 20.3 %copy-start.10 = (f32[2,2]{1,0:T(2,128)S(1)}, f32[2,2]{1,0:T(2,128)}, u32[]{:S(2)}) copy-start(f32[2,2]{1,0:T(2,128)} %param.20) | copy-start | bytes 52
  7.2 35.3 %all-gather.7.cloned.1.call-start = ((), (), s32[]{:S(2)}) async-start(), calls=%async_computation.1 | async-start | bytes 2752512 | tf_op jit(solution)/shard_map/all_gather | solution.py:70
  47.8 2.8 copy-start.1
  47.8 2.8 copy-start.9
  50.6 52.4 %all-gather.9.cloned.1.call-start = ((), (), s32[]{:S(2)}) async-start(), calls=%async_computation.3 | async-start | bytes 2752512 | tf_op jit(solution)/shard_map/while/body/eval_jaxpr/all_gather | solution.py:134
  50.7 6.0 %collective-permute-start = (bf16[2,64,3584]{2,1,0:T(8,128)(2,1)S(1)}, bf16[2,64,3584]{2,1,0:T(8,128)(2,1)}, u32[]{:S(2)}, u32[]{:S(2)}) collective-permute-start(bf16[2,64,3584]{2,1,0:T(8,128)(2,1)S(1)} %broadcast_select_fusion.2), channel_id=1, source_target_pairs={{16,0},{17,1},{18,2},{19,3},{20,4},{21,5},{22,6},{23,7},{24,8},{25... | collective-permute-start | bytes 2752520 | tf_op jit(solution)/shard_map/while/body/eval_jaxpr/ppermute | solution.py:15
  52.0 3.6 copy-start.3
  52.0 3.6 copy-start.4
  55.6 1.8 copy-start.7
  59.1 1.3 copy-start.5
  63.0 1.7 copy-start.2
  104.8 2.1 copy-start
  110.3 53.5 %all-gather.9.cloned.1.call-start = ((), (), s32[]{:S(2)}) async-start(), calls=%async_computation.3 | async-start | bytes 2752512 | tf_op jit(solution)/shard_map/while/body/eval_jaxpr/all_gather | solution.py:134
  111.6 6.0 %collective-permute-start = (bf16[2,64,3584]{2,1,0:T(8,128)(2,1)S(1)}, bf16[2,64,3584]{2,1,0:T(8,128)(2,1)}, u32[]{:S(2)}, u32[]{:S(2)}) collective-permute-start(bf16[2,64,3584]{2,1,0:T(8,128)(2,1)S(1)} %broadcast_select_fusion.2), channel_id=1, source_target_pairs={{16,0},{17,1},{18,2},{19,3},{20,4},{21,5},{22,6},{23,7},{24,8},{25... | collective-permute-start | bytes 2752520 | tf_op jit(solution)/shard_map/while/body/eval_jaxpr/ppermute | solution.py:15
  112.9 3.6 copy-start.3
  112.9 3.6 copy-start.4
  116.5 1.8 copy-start.7
  120.0 1.3 copy-start.5
  121.3 5.0 copy-start.8
  133.0 2.4 copy-start.2
  165.8 2.1 copy-start
  171.2 53.0 %all-gather.9.cloned.1.call-start = ((), (), s32[]{:S(2)}) async-start(), calls=%async_computation.3 | async-start | bytes 2752512 | tf_op jit(solution)/shard_map/while/body/eval_jaxpr/all_gather | solution.py:134
  172.5 6.0 %collective-permute-start = (bf16[2,64,3584]{2,1,0:T(8,128)(2,1)S(1)}, bf16[2,64,3584]{2,1,0:T(8,128)(2,1)}, u32[]{:S(2)}, u32[]{:S(2)}) collective-permute-start(bf16[2,64,3584]{2,1,0:T(8,128)(2,1)S(1)} %broadcast_select_fusion.2), channel_id=1, source_target_pairs={{16,0},{17,1},{18,2},{19,3},{20,4},{21,5},{22,6},{23,7},{24,8},{25... | collective-permute-start | bytes 2752520 | tf_op jit(solution)/shard_map/while/body/eval_jaxpr/ppermute | solution.py:15
  173.8 3.6 copy-start.3
  173.8 3.6 copy-start.4
  177.4 1.8 copy-start.7
  180.9 1.3 copy-start.5
  182.2 5.0 copy-start.8
  193.9 2.4 copy-start.2
  226.2 2.1 copy-start
  231.6 272.1 %reduce-scatter.4.cloned.1.call-start = ((), (), s32[]{:S(2)}) async-start(), calls=%async_computation.2 | async-start | bytes 16515072
  231.6 2.1 copy-start.6
  266.3 0.7 copy-start.11
Sparse Core Ops, SparseCore 0:
  9.5 32.8 all-gather.6
  63.2 39.7 all-gather.8
  133.2 30.6 all-gather.8
  194.1 30.1 all-gather.8
  266.5 237.1 reduce-scatter.3
